TPU v7x, 32 devices: a whole 2x2x4 slice. The times are simulated.
32 devices in a mesh: member: 2 (over x), graph: 8 (over z, y), chan: 2 (over core).
Axes of the slice: x: 2, y: 2, z: 4, core: 2. Of those that a mesh axis runs over, the one named last changes fastest.
Arguments:
- grid_state: bfloat16 [16384, 256], P(('member', 'graph')), parts along dimension 0, may hold values from -6 to 6
- w_src: bfloat16 [256, 512], P(None, 'chan'), may hold values from -0.375 to 0.375
- bias_src: float32 [512], P('chan'), may hold values from -3 to 3
- mesh_embed: bfloat16 [5120, 512], P('graph', 'chan'), may hold values from -6 to 6
- w_node: bfloat16 [512, 512], P('chan'), may hold values from -0.25 to 0.25
- w_dec: bfloat16 [512, 256], P('chan'), may hold values from -0.125 to 0.125
- slot_src: int32 [8, 8, 1024], P('graph'), may hold values from 0 to 1023, as said below
- slot_dst: int32 [8, 8, 1024], P(None, 'graph'), may hold values from 0 to 639, as said below
- slot_count: int32 [8, 8], replicated, may hold values from 1 to 1024, as said below
Outputs:
- grid_out: bfloat16 [16384, 256], P(('member', 'graph'), 'chan'), parts along dimension 0
There are 2 independent parts, one for each index of `member`. A program takes and returns all parts, laid end to end along the dimension named above; an argument that names none is the same for every part. Nothing has to cross between parts.
Inputs may be any that keep to these rules, and one draw needn't show every extreme that they name: `slot_src`: slots at or past the live count hold arbitrary values in the same range. `slot_dst`: slots at or past the live count hold arbitrary values in the same range. slot_count[s, d] counts the live leading slots of the 1024 from shard s to shard d; in every draw some receiving shard has all 1024 slots live from every sender.
All inputs are finite; a program needn't handle non-finite values.
Results may differ from a plain program's by a relative error of at most 0.0056.
Values may be sent and summed in bfloat16 or wider, within the bound.
A program may use at most 64 MiB of HBM per device.

v0:
```python
import math

import jax
import jax.numpy as jnp
from jax import lax
from jax.sharding import PartitionSpec as P


def edge_network(source_rows, w_src, bias_src):
    return jax.nn.silu(
        jnp.dot(source_rows, w_src, preferred_element_type=jnp.float32) + bias_src
    ).astype(jnp.bfloat16)


def segment_rows(values, indices, usable, row_count):
    slot_total = values.shape[0]
    width = values.shape[1]
    block_len = math.gcd(slot_total, 2048)
    block_count = slot_total // block_len
    targets = jnp.where(usable, indices, -1).reshape(block_count, block_len)
    pieces = values.reshape(block_count, block_len, width)
    row_ids = jnp.arange(row_count, dtype=jnp.int32)

    def add_block(summed, scan_item):
        row_target, piece_vals = scan_item
        one_hot = (row_ids[:, None] == row_target[None, :]).astype(jnp.bfloat16)
        return (summed + jnp.dot(one_hot, piece_vals, preferred_element_type=jnp.float32), None)

    result, unused = lax.scan(
        add_block, jnp.zeros((row_count, width), jnp.float32), (targets, pieces)
    )
    return result


def on_device(
    grid_state, w_src, bias_src, mesh_embed, w_node, w_dec, slot_src, slot_dst, slot_count
):
    peers = lax.axis_size("graph")
    own_index = lax.axis_index("graph")
    core_index = lax.axis_index("chan")
    capacity = slot_src.shape[2]
    positions = jnp.arange(capacity, dtype=jnp.int32)
    grid_rows = grid_state.shape[0]
    mesh_rows = mesh_embed.shape[0]
    sent_counts = lax.dynamic_slice_in_dim(slot_count, own_index, 1, 0)[0]
    recv_counts = lax.dynamic_slice_in_dim(slot_count, own_index, 1, 1)[:, 0]
    half_slots = capacity // 2
    chosen = lax.dynamic_slice_in_dim(slot_src[0], core_index * half_slots, half_slots, 1)
    picked = jnp.take(grid_state, chosen.reshape(-1), axis=0).reshape(
        peers, half_slots, grid_state.shape[1]
    )
    arrived = lax.all_to_all(picked, "graph", split_axis=0, concat_axis=0, tiled=True)
    joined = lax.all_gather(arrived, "chan", axis=1, tiled=True)
    messages = edge_network(joined.reshape(peers * capacity, grid_state.shape[1]), w_src, bias_src)
    arrive_ok = (positions[None, :] < recv_counts[:, None]).reshape(-1)
    dst_rows = slot_dst[:, 0, :].reshape(-1)
    aggregate = segment_rows(messages, dst_rows, arrive_ok, mesh_rows)
    partial_hidden = jnp.dot(
        aggregate.astype(jnp.bfloat16), w_node, preferred_element_type=jnp.float32
    )
    hidden_pre = lax.psum_scatter(partial_hidden, "chan", scatter_dimension=1, tiled=True)
    latent = (mesh_embed.astype(jnp.float32) + jax.nn.silu(hidden_pre)).astype(jnp.bfloat16)
    partial_proj = jnp.dot(latent, w_dec, preferred_element_type=jnp.float32)
    projected = lax.psum_scatter(partial_proj, "chan", scatter_dimension=1, tiled=True).astype(
        jnp.bfloat16
    )
    returned = jnp.take(projected, dst_rows, axis=0).reshape(peers, capacity, projected.shape[1])
    came_back = lax.all_to_all(returned, "graph", split_axis=0, concat_axis=0, tiled=True).reshape(
        peers * capacity, projected.shape[1]
    )
    send_ok = (positions[None, :] < sent_counts[:, None]).reshape(-1)
    decoded = segment_rows(came_back, slot_src[0].reshape(-1), send_ok, grid_rows)
    width_half = decoded.shape[1]
    own_cols = lax.dynamic_slice_in_dim(grid_state, core_index * width_half, width_half, 1)
    return (own_cols.astype(jnp.float32) + decoded).astype(jnp.bfloat16)


def solution(mesh):
    placed = (
        P(("member", "graph"), None),
        P(None, "chan"),
        P("chan"),
        P("graph", "chan"),
        P("chan", None),
        P("chan", None),
        P("graph", None, None),
        P(None, "graph", None),
        P(),
    )
    return jax.shard_map(
        on_device,
        mesh=mesh,
        in_specs=placed,
        out_specs=P(("member", "graph"), "chan"),
        check_vma=False,
    )
```

profile of v0, /device:TPU:0, one launch (start us, length us, event | category | flops | bytes accessed | tf_op | source)
XLA Modules:
  0.0 227.8 jit_solution(10964538326283773564)
XLA Ops:
  6.5 0.0 copy-start
  6.5 0.0 all-gather.2.cloned.1.call-start
  6.5 0.8 dynamic-slice_bitcast_fusion
  7.3 0.7 compare_and_fusion.1
  8.1 14.1 %gather_fusion = bf16[4096,256]{1,0:T(8,128)(2,1)S(1)} fusion(bf16[1024,256]{1,0:T(8,128)(2,1)} %param.13, s32[4096]{0:T(1024)S(1)} %broadcast_clamp_fusion.1), kind=kCustom, calls=%fused_computation | custom fusion | bytes 4210688 | tf_op jit(solution)/shard_map/jit(_take)/gather | solution.py:49
  22.2 1.0 broadcast_select_fusion
  23.2 55.4 %all_to_all.10 = bf16[8,512,256]{2,1,0:T(8,128)(2,1)} all-to-all(bf16[8,512,256]{2,1,0:T(8,128)(2,1)S(1)} %broadcast_select_fusion), channel_id=1, replica_groups=mesh['member'=2,'graph'=8,'chan'=2] {'graph'}, dimensions={0} | all-to-all | bytes 4194304 | tf_op jit(solution)/shard_map/all_to_all | solution.py:52
  78.6 0.0 copy-start.4
  78.6 0.0 copy-start.3
  78.6 0.0 copy-start.2
  78.6 0.0 copy-start.6
  78.6 0.0 copy-start.8
  78.6 0.0 all-gather.2.cloned.1.call-update
  78.7 0.0 reduce-scatter.3.cloned.1.call-start
  78.7 0.6 copy-done.4
  79.3 0.2 dynamic-slice_reduce_fusion
  79.5 0.0 copy-done.3
  79.6 0.1 lt.111
  79.6 0.1 broadcast_bitcast_fusion.1
  79.7 0.1 lt.117
  79.8 0.1 broadcast_bitcast_fusion
  79.9 0.0 copy-done.2
  79.9 0.1 reduce.2
  80.1 11.4 %all-gather.2.cloned.1.call-done = bf16[8,1024,256]{2,1,0:T(8,128)(2,1)} async-done(((bf16[8,512,256]{2,1,0:T(8,128)(2,1)}), bf16[8,1024,256]{2,1,0:T(8,128)(2,1)}) %all-gather.2.cloned.1.call-update) | async-done | bytes 4194320 | tf_op jit(solution)/shard_map/all_gather | solution.py:53
  91.5 0.0 copy-done.6
  91.5 0.0 copy-done.8
  91.5 6.1 %multiply_convert_fusion = bf16[8192,256]{1,0:T(8,128)(2,1)} fusion(bf16[8192,256]{1,0:T(8,128)(2,1)} %bitcast.63, bf16[256,256]{1,0:T(8,128)(2,1)S(1)} %copy-done.6, f32[256]{0:T(256)S(1)} %copy-done.8), kind=kOutput, calls=%fused_computation.21 | convolution fusion | flops 1086324736 | bytes 8520704 | tf_op jit(solution)/shard_map/dot_general | solution.py:11
  97.6 9.2 %while.22 = (s32[]{:T(128)}, f32[640,256]{1,0:T(8,128)S(1)}, s32[4,2048]{1,0:T(4,128)S(1)}, bf16[4,2048,256]{2,1,0:T(8,128)(2,1)}, s32[]{:T(128)}, /*index=5*/s32[]{:T(128)}) while((s32[]{:T(128)}, f32[640,256]{1,0:T(8,128)S(1)}, s32[4,2048]{1,0:T(4,128)S(1)}, bf16[4,2048,256]{2,1,0:T(8,128)(2,1)}, s32[]{:T(128)}, ...), condition=%wide.region_1.2_spmd.clone, body=%wide.region_0.1_spmd.clone.sunk | while | flops 672727040 | bytes 2384467 | solution.py:29
  97.6 2.3 fusion.30
  99.9 2.3 fusion.30
  102.2 2.3 fusion.30
  104.5 2.3 fusion.30
  106.8 0.0 copy-start.5
  106.8 0.0 copy-start.7
  106.8 0.0 copy-done
  106.9 1.4 fusion.16
  108.3 0.0 reduce-scatter.3.cloned.1.call-update
  108.3 0.0 reduce-scatter.5.cloned.1.call-start
  108.4 9.9 %reduce-scatter.3.cloned.1.call-done = f32[640,256]{1,0:T(8,128)} async-done(((f32[640,512]{1,0:T(8,128)}), f32[640,256]{1,0:T(8,128)}) %reduce-scatter.3.cloned.1.call-update) | async-done | bytes 655376 | tf_op jit(solution)/shard_map/reduce_scatter | solution.py:61
  118.2 0.0 copy-done.5
  118.2 0.0 copy-done.7
  118.2 2.2 fusion.18
  120.5 0.0 reduce-scatter.5.cloned.1.call-update
  120.6 9.4 %reduce-scatter.5.cloned.1.call-done = f32[640,128]{1,0:T(8,128)} async-done(((f32[640,256]{1,0:T(8,128)}), f32[640,128]{1,0:T(8,128)}) %reduce-scatter.5.cloned.1.call-update) | async-done | bytes 327696 | tf_op jit(solution)/shard_map/reduce_scatter | solution.py:64
  130.0 1.0 convert_element_type.28
  131.0 24.0 %gather_fusion.1 = bf16[8192,128]{1,0:T(8,128)(2,1)S(1)} fusion(bf16[640,128]{1,0:T(8,128)(2,1)S(1)} %convert_element_type.28, s32[8192]{0:T(1024)S(1)} %broadcast_clamp_fusion), kind=kCustom, calls=%fused_computation.1 | custom fusion | bytes 4227072 | tf_op jit(solution)/shard_map/jit(_take)/gather | solution.py:67
  155.0 4.0 %broadcast_select_fusion.1 = bf16[8,1024,128]{2,1,0:T(8,128)(2,1)} fusion(bf16[8,1024,128]{2,1,0:T(8,128)(2,1)S(1)} %bitcast.51, pred[8,1024]{1,0:T(8,128)(4,1)S(1)} %compare_and_fusion), kind=kLoop, calls=%fused_computation.23 | loop fusion | flops 1048576 | bytes 4202496 | tf_op jit(solution)/shard_map/jit(_take)/select_n | solution.py:67
  159.0 5.7 %all-to-all-start.1 = ((bf16[8,1024,128]{2,1,0:T(8,128)(2,1)}), bf16[8,1024,128]{2,1,0:T(8,128)(2,1)S(1)}, u32[]{:S(2)}, u32[]{:S(2)}) async-start(bf16[8,1024,128]{2,1,0:T(8,128)(2,1)} %broadcast_select_fusion.1), calls=%async_computation.3 | async-start | bytes 4194304 | tf_op jit(solution)/shard_map/all_to_all | solution.py:68
  164.7 48.7 %all-to-all-done.1 = bf16[8,1024,128]{2,1,0:T(8,128)(2,1)S(1)} async-done(((bf16[8,1024,128]{2,1,0:T(8,128)(2,1)}), bf16[8,1024,128]{2,1,0:T(8,128)(2,1)S(1)}, u32[]{:S(2)}, u32[]{:S(2)}) %all-to-all-start.1) | async-done | bytes 2097184 | tf_op jit(solution)/shard_map/all_to_all | solution.py:68
  213.5 0.0 copy-start.1
  213.5 7.0 %while.23 = (s32[]{:T(128)}, f32[1024,128]{1,0:T(8,128)S(1)}, s32[4,2048]{1,0:T(4,128)S(1)}, bf16[4,2048,128]{2,1,0:T(8,128)(2,1)S(1)}, s32[]{:T(128)}, /*index=5*/s32[]{:T(128)}) while((s32[]{:T(128)}, f32[1024,128]{1,0:T(8,128)S(1)}, s32[4,2048]{1,0:T(4,128)S(1)}, bf16[4,2048,128]{2,1,0:T(8,128)(2,1)S(1)}, s32[]{:T(128)}, ...), condition=%wide.region_5.6_spmd.clone, body=%wide.region_4.5_spmd.clone.sunk | while | flops 539230208 | bytes 1597527 | solution.py:29
  213.5 1.7 fusion.32
  215.3 1.7 fusion.32
  217.0 1.7 fusion.32
  218.8 1.7 fusion.32
  220.5 0.0 copy-done.1
  220.5 0.8 add_convert_fusion.1
  (24 shorter events, 0.3 us)
Async XLA Ops:
  6.5 100.3 %copy-start = (bf16[256,512]{1,0:T(8,128)(2,1)S(1)}, bf16[256,512]{1,0:T(8,128)(2,1)}, u32[]{:S(2)}) copy-start(bf16[256,512]{1,0:T(8,128)(2,1)} %param.17) | copy-start | bytes 786436
  6.5 85.0 %all-gather.2.cloned.1.call-start = ((), (), s32[]{:S(2)}) async-start(), calls=%async_computation.4 | async-start | bytes 6291456 | tf_op jit(solution)/shard_map/all_gather | solution.py:53
  78.6 0.7 copy-start.4
  78.6 0.9 copy-start.3
  78.6 1.3 copy-start.2
  78.6 12.9 %copy-start.6 = (bf16[256,256]{1,0:T(8,128)(2,1)S(1)}, bf16[256,256]{1,0:T(8,128)(2,1)}, u32[]{:S(2)}) copy-start(bf16[256,256]{1,0:T(8,128)(2,1)} %param.14) | copy-start | bytes 393220
  78.6 12.9 %copy-start.8 = (f32[256]{0:T(256)S(1)}, f32[256]{0:T(256)}, u32[]{:S(2)}) copy-start(f32[256]{0:T(256)} %param.15) | copy-start | bytes 3076
  78.7 39.5 %reduce-scatter.3.cloned.1.call-start = ((), (), s32[]{:S(2)}) async-start(), calls=%async_computation.5 | async-start | bytes 1966080 | tf_op jit(solution)/shard_map/reduce_scatter | solution.py:61
  106.8 11.4 %copy-start.5 = (bf16[640,256]{1,0:T(8,128)(2,1)S(1)}, bf16[640,256]{1,0:T(8,128)(2,1)}, u32[]{:S(2)}) copy-start(bf16[640,256]{1,0:T(8,128)(2,1)} %param.16) | copy-start | bytes 983044
  106.8 11.4 %copy-start.7 = (bf16[256,256]{1,0:T(8,128)(2,1)S(1)}, bf16[256,256]{1,0:T(8,128)(2,1)}, u32[]{:S(2)}) copy-start(bf16[256,256]{1,0:T(8,128)(2,1)} %param.18) | copy-start | bytes 393220
  108.3 21.7 %reduce-scatter.5.cloned.1.call-start = ((), (), s32[]{:S(2)}) async-start(), calls=%async_computation.6 | async-start | bytes 983040 | tf_op jit(solution)/shard_map/reduce_scatter | solution.py:64
  159.0 54.5 %all-to-all-start.1 = ((bf16[8,1024,128]{2,1,0:T(8,128)(2,1)}), bf16[8,1024,128]{2,1,0:T(8,128)(2,1)S(1)}, u32[]{:S(2)}, u32[]{:S(2)}) async-start(bf16[8,1024,128]{2,1,0:T(8,128)(2,1)} %broadcast_select_fusion.1), calls=%async_computation.3 | async-start | bytes 4194304 | tf_op jit(solution)/shard_map/all_to_all | solution.py:68
  213.5 7.0 %copy-start.1 = (bf16[1024,256]{1,0:T(8,128)(2,1)S(1)}, bf16[1024,256]{1,0:T(8,128)(2,1)}, u32[]{:S(2)}) copy-start(bf16[1024,256]{1,0:T(8,128)(2,1)} %param.13) | copy-start | bytes 1572868
Sparse Core Ops, SparseCore 0:
  78.8 12.6 all-gather.1
  108.4 9.7 reduce-scatter.2
  120.6 9.3 reduce-scatter.4
where the time goes:
time: 228 us
  waiting for transfers between devices  79.5 us (35%)
  blocking collectives  55.4 us (24%)
  local copies, waits for them, and re-layouts  40.2 us (18%)
  matrix products  25.6 us (11%)
  between operations  13.3 us (6%)
  other arithmetic  7.66 us (3%)
  starting transfers between devices  5.81 us (3%)
    all_to_all x1, blocking collectives, on_device(): lax.all_to_all(picked, 'graph', split_axis=0, concat_axis=0, tiled=True)  55.4 us
    all_to_all x1, waiting for transfers between devices, on_device(): lax.all_to_all(returned, 'graph', split_axis=0, concat_axis=0, tiled=True)  48.7 us
    gather x1, local copies, waits for them, and re-layouts, on_device(): jnp.take(projected, dst_rows, axis=0)  24 us
    dot_general x8, matrix products, add_block(): jnp.dot(one_hot, piece_vals, preferred_element_type=jnp.float32)  15.9 us
    gather x1, local copies, waits for them, and re-layouts, on_device(): jnp.take(grid_state, chosen.reshape(-1), axis=0)  14.1 us
    all_gather x1, waiting for transfers between devices, on_device(): joined = lax.all_gather(arrived, 'chan', axis=1, tiled=True)  11.4 us
    reduce_scatter x1, waiting for transfers between devices, on_device(): lax.psum_scatter(partial_hidden, 'chan', scatter_dimension=1, tiled=True)  9.86 us
    reduce_scatter x1, waiting for transfers between devices, on_device(): lax.psum_scatter(partial_proj, 'chan', scatter_dimension=1, tiled=True)  9.43 us
  transfers between devices with their start and end apart: 4, of which 4 were waited for; matrix products, arithmetic and copies ran while one was open for 0% of the time, Pallas kernels for 0%

commit v1 on v0

--- a/solution.py
+++ b/solution.py
@@ -1,9 +1,16 @@
+import functools
 import math
 
 import jax
 import jax.numpy as jnp
 from jax import lax
+from jax.experimental import pallas as pl
+from jax.experimental.pallas import tpu as pltpu
 from jax.sharding import PartitionSpec as P
+
+VMEM_BUDGET = 48 * 2**20
+MESH = pl.DeviceIdType.MESH
+NT = (((1,), (1,)), ((), ()))
 
 
 def edge_network(source_rows, w_src, bias_src):
@@ -75,6 +82,337 @@
     return (own_cols.astype(jnp.float32) + decoded).astype(jnp.bfloat16)
 
 
+def silu(v):
+    half = 0.5 * v
+    return half + half * jnp.tanh(half)
+
+
+def one_hot(first, rows, indices):
+    row_ids = lax.broadcasted_iota(jnp.int32, (rows, indices.shape[1]), 0) + first
+    return jnp.where(row_ids == indices, 1.0, 0.0).astype(jnp.bfloat16)
+
+
+def graph_kernel(
+    peers,
+    x_ref, w_src_ref, bias_ref, embed_ref, w_node_ref, w_dec_ref, src_ref, dst_ref,
+    out_ref,
+    x_all, src_in, dst_in, w_src_all, bias_all, embed_all, w_node_all, w_dec_all,
+    enc, dec, hot, agg, proj, proj_all, total,
+    local_sem, par_send, par_recv, idx_send, idx_recv,
+    xz_send, xy_send, xi_recv, xm_send, xm_recv,
+    pz_send, pz_recv, py_send, py_recv, pm_send, pm_recv, pr_send, pr_recv,
+):
+    lines = peers // 2
+    me = lax.axis_index("graph")
+    core = lax.axis_index("chan")
+    mate = 1 - core
+    line, side = me // 2, me % 2
+    other = line * 2 + (1 - side)
+    grid_rows, chans = x_ref.shape
+    half_grid = grid_rows // 2
+    mesh_rows = embed_ref.shape[0]
+    half_mesh = mesh_rows // 2
+    cols = chans // 2
+    tile = enc.shape[3]
+    tiles = grid_rows // tile
+
+    def remote(src, dst, send, recv, graph, chan):
+        return pltpu.make_async_remote_copy(
+            src_ref=src, dst_ref=dst, send_sem=send, recv_sem=recv,
+            device_id={"graph": graph, "chan": chan}, device_id_type=MESH,
+        )
+
+    barrier = pltpu.get_barrier_semaphore()
+    for step in range(peers):
+        for chan in range(2):
+            if step == 0 and chan == 0:
+                continue
+            pl.semaphore_signal(
+                barrier, inc=1,
+                device_id={"graph": (me + step) % peers, "chan": (core + chan) % 2},
+                device_id_type=MESH,
+            )
+    locals_ = [
+        pltpu.make_async_copy(x_ref, x_all.at[me], local_sem.at[0]),
+        pltpu.make_async_copy(w_src_ref, w_src_all.at[core], local_sem.at[1]),
+        pltpu.make_async_copy(bias_ref, bias_all.at[core], local_sem.at[2]),
+        pltpu.make_async_copy(
+            embed_ref.at[pl.ds(pl.multiple_of(core * half_mesh, half_mesh), half_mesh)],
+            embed_all.at[core], local_sem.at[3]),
+        pltpu.make_async_copy(w_node_ref, w_node_all.at[core], local_sem.at[4]),
+        pltpu.make_async_copy(w_dec_ref, w_dec_all.at[core], local_sem.at[5]),
+        pltpu.make_async_copy(src_ref.at[me], src_in.at[me], local_sem.at[6]),
+        pltpu.make_async_copy(dst_ref.at[me], dst_in.at[me], local_sem.at[7]),
+    ]
+    for copy in locals_:
+        copy.start()
+    pl.semaphore_wait(barrier, 2 * peers - 1)
+
+    idx_copies = []
+    for step in range(1, peers):
+        to = (me + step) % peers
+        for at, (ref, into) in enumerate(((src_ref, src_in), (dst_ref, dst_in))):
+            copy = remote(
+                ref.at[to], into.at[me], idx_send.at[at, step], idx_recv.at[at, step], to, core
+            )
+            copy.start()
+            idx_copies.append(copy)
+
+    def x_block(shard, half):
+        return x_all.at[shard, pl.ds(pl.multiple_of(half * half_grid, half_grid), half_grid)]
+
+    def x_copy(shard, send, recv_at, graph):
+        ref = x_block(shard, core)
+        return remote(ref, ref, send, xi_recv.at[recv_at], graph, core)
+
+    own_half = x_ref.at[pl.ds(pl.multiple_of(core * half_grid, half_grid), half_grid)]
+    y_copies = [remote(own_half, x_block(me, core), xy_send.at[0], xi_recv.at[0], other, core)]
+    y_copies[0].start()
+    z_copies = {}
+    z_order = [k for pair in zip(range(1, lines), range(lines - 1, 0, -1)) for k in pair]
+    z_order = list(dict.fromkeys(z_order))
+    for k in z_order:
+        to = ((line + k) % lines) * 2 + side
+        z_copies[k] = remote(
+            own_half, x_block(me, core), xz_send.at[k], xi_recv.at[k], to, core
+        )
+        z_copies[k].start()
+
+    mate_rows = pl.ds(pl.multiple_of(mate * half_mesh, half_mesh), half_mesh)
+    par_copies = [
+        remote(w_src_ref, w_src_all.at[core], par_send.at[0], par_recv.at[0], me, mate),
+        remote(bias_ref, bias_all.at[core], par_send.at[1], par_recv.at[1], me, mate),
+        remote(embed_ref.at[mate_rows], embed_all.at[core], par_send.at[2], par_recv.at[2], me, mate),
+        remote(w_node_ref, w_node_all.at[core], par_send.at[3], par_recv.at[3], me, mate),
+        remote(w_dec_ref, w_dec_all.at[core], par_send.at[4], par_recv.at[4], me, mate),
+    ]
+    for copy in par_copies:
+        copy.start()
+    for copy in locals_:
+        copy.wait()
+    for copy in idx_copies:
+        copy.wait()
+
+    def build_enc(shard, carry):
+        hot[: half_mesh, :] = one_hot(core * half_mesh, half_mesh, dst_ref[shard])
+        for t in range(tiles):
+            picks = one_hot(t * tile, tile, src_in[shard])
+            enc[shard, t] = lax.dot_general(
+                hot[: half_mesh, :], picks, NT, preferred_element_type=jnp.float32
+            ).astype(jnp.bfloat16)
+        return carry
+
+    def build_dec(shard, carry):
+        hot[...] = one_hot(0, mesh_rows, dst_in[shard])
+        for t in range(grid_rows // 256):
+            picks = one_hot(t * 256, 256, src_ref[shard])
+            dec[shard, t * 256 : (t + 1) * 256, :] = lax.dot_general(
+                picks, hot[...], NT, preferred_element_type=jnp.float32
+            ).astype(jnp.bfloat16)
+        return carry
+
+    def shard_of(event):
+        if event == 0:
+            return other
+        k = event if event < lines else event - lines + 1
+        from_line = (line + lines - k) % lines
+        return from_line * 2 + (side if event < lines else 1 - side)
+
+    mate_copies = {}
+
+    def relay(event):
+        shard = shard_of(event)
+        x_copy(shard, xy_send.at[0], event, other).wait_recv()
+        if 0 < event < lines:
+            copy = x_copy(shard, xy_send.at[event], lines - 1 + event, other)
+            copy.start()
+            y_copies.append(copy)
+        ref = x_block(shard, core)
+        copy = remote(ref, ref, xm_send.at[event], xm_recv.at[event], me, mate)
+        copy.start()
+        mate_copies[event] = copy
+
+    def encode(shard, t):
+        for h in range(2):
+            pre = jnp.dot(
+                x_all[shard, t * tile : (t + 1) * tile, :], w_src_all[h],
+                preferred_element_type=jnp.float32,
+            ) + bias_all[h]
+            part = jnp.dot(
+                enc[shard, t], silu(pre).astype(jnp.bfloat16), preferred_element_type=jnp.float32
+            )
+            agg[h] += part
+
+    def encode_event(event):
+        mate_copies[event].wait_recv()
+        for t in range(tiles):
+            encode(shard_of(event), t)
+
+    lax.fori_loop(0, peers // 2, build_enc, 0)
+    for k in z_order[:2]:
+        relay(k)
+    lax.fori_loop(peers // 2, peers, build_enc, 0)
+    relay(0)
+    for copy in par_copies:
+        copy.wait()
+    agg[...] = jnp.zeros_like(agg)
+    for t in range(tiles):
+        encode(me, t)
+    for k in z_order[2:]:
+        relay(k)
+    for event in [0] + z_order:
+        encode_event(event)
+    early = peers // 2
+    pieces = [early * i // (lines - 1) for i in range(lines)]
+    for i, k in enumerate(z_order):
+        lax.fori_loop(pieces[i], pieces[i + 1], build_dec, 0)
+        relay(lines - 1 + k)
+    for k in z_order:
+        encode_event(lines - 1 + k)
+
+    hidden = sum(
+        jnp.dot(agg[h].astype(jnp.bfloat16), w_node_all[h], preferred_element_type=jnp.float32)
+        for h in range(2)
+    )
+    width = hidden.shape[1] // 2
+    projected = sum(
+        jnp.dot(
+            (
+                embed_all[h].astype(jnp.float32) + silu(hidden[:, h * width : (h + 1) * width])
+            ).astype(jnp.bfloat16),
+            w_dec_all[h], preferred_element_type=jnp.float32,
+        )
+        for h in range(2)
+    ).astype(jnp.bfloat16)
+    for h in range(2):
+        proj[h] = projected[:, h * cols : (h + 1) * cols]
+
+    my_rows = pl.ds(pl.multiple_of(core * half_mesh, half_mesh), half_mesh)
+    own_copy = pltpu.make_async_copy(proj.at[core], proj_all.at[me, my_rows], local_sem.at[0])
+    own_copy.start()
+    into = proj_all.at[me, my_rows]
+    p_copies = []
+    for flip in range(2):
+        chan = (core + flip) % 2
+        copy = remote(proj.at[chan], into, py_send.at[flip], py_recv.at[flip], other, chan)
+        copy.start()
+        p_copies.append(copy)
+    for k in z_order:
+        to = ((line + k) % lines) * 2 + side
+        for flip in range(2):
+            chan = (core + flip) % 2
+            copy = remote(
+                proj.at[chan], into, pz_send.at[k, flip], pz_recv.at[k, flip], to, chan
+            )
+            copy.start()
+            p_copies.append(copy)
+    mate_copy = remote(proj.at[mate], into, pm_send.at[0], pm_recv.at[0], me, mate)
+    mate_copy.start()
+    p_copies.append(mate_copy)
+
+    def decode(shard):
+        for t in range(2):
+            rows = slice(t * half_grid, (t + 1) * half_grid)
+            total[rows, :] += jnp.dot(
+                dec[shard, rows, :], proj_all[shard], preferred_element_type=jnp.float32
+            )
+
+    pieces = [early + (peers - early) * i // (lines - 1) for i in range(lines)]
+    r_copies = []
+    for i, k in enumerate(z_order):
+        lax.fori_loop(pieces[i], pieces[i + 1], build_dec, 0)
+        shard = ((line + lines - k) % lines) * 2 + side
+        for flip in range(2):
+            remote(proj.at[core], into, pz_send.at[k, flip], pz_recv.at[k, flip], me, mate).wait_recv()
+        copy = remote(
+            proj_all.at[shard], proj_all.at[shard], pr_send.at[k], pr_recv.at[k], other, core
+        )
+        copy.start()
+        r_copies.append(copy)
+    own_cols = x_ref[:, pl.ds(pl.multiple_of(core * cols, cols), cols)]
+    total[...] = own_cols.astype(jnp.float32)
+    own_copy.wait()
+    mate_copy.wait_recv()
+    decode(me)
+    for copy in p_copies[:2]:
+        copy.wait_recv()
+    decode(other)
+    for k in z_order:
+        decode(((line + lines - k) % lines) * 2 + side)
+    for i, k in enumerate(z_order):
+        r_copies[i].wait_recv()
+        decode(((line + lines - k) % lines) * 2 + (1 - side))
+    out_ref[...] = total[...].astype(jnp.bfloat16)
+
+    for copy in y_copies + list(z_copies.values()) + list(mate_copies.values()) + p_copies + r_copies:
+        copy.wait_send()
+
+
+def fused(grid_state, w_src, bias_src, mesh_embed, w_node, w_dec, slot_src, slot_dst, slot_count):
+    peers = lax.axis_size("graph")
+    own_index = lax.axis_index("graph")
+    capacity = slot_src.shape[2]
+    positions = jnp.arange(capacity, dtype=jnp.int32)
+    sent = lax.dynamic_slice_in_dim(slot_count, own_index, 1, 0)[0]
+    received = lax.dynamic_slice_in_dim(slot_count, own_index, 1, 1)[:, 0]
+    src = jnp.where(positions < sent[:, None], slot_src[0], -1)[:, None, :]
+    dst = jnp.where(positions < received[:, None], slot_dst[:, 0, :], -1)[:, None, :]
+    grid_rows, chans = grid_state.shape
+    mesh_rows = mesh_embed.shape[0]
+    hidden = w_src.shape[1]
+    lines = peers // 2
+    bf16, f32 = jnp.bfloat16, jnp.float32
+    dma = pltpu.SemaphoreType.DMA
+    vmem = pl.BlockSpec(memory_space=pltpu.VMEM)
+    tile = grid_rows // 2
+    return pl.pallas_call(
+        functools.partial(graph_kernel, peers),
+        out_shape=jax.ShapeDtypeStruct((grid_rows, chans // 2), bf16),
+        in_specs=[vmem] * 8,
+        out_specs=vmem,
+        scratch_shapes=[
+            pltpu.VMEM((peers, grid_rows, chans), bf16),
+            pltpu.VMEM((peers, 1, capacity), jnp.int32),
+            pltpu.VMEM((peers, 1, capacity), jnp.int32),
+            pltpu.VMEM((2,) + w_src.shape, bf16),
+            pltpu.VMEM((2, 1, hidden), f32),
+            pltpu.VMEM((2, mesh_rows // 2, hidden), bf16),
+            pltpu.VMEM((2,) + w_node.shape, bf16),
+            pltpu.VMEM((2,) + w_dec.shape, bf16),
+            pltpu.VMEM((peers, grid_rows // tile, mesh_rows // 2, tile), bf16),
+            pltpu.VMEM((peers, grid_rows, mesh_rows), bf16),
+            pltpu.VMEM((mesh_rows, capacity), bf16),
+            pltpu.VMEM((2, mesh_rows // 2, hidden), f32),
+            pltpu.VMEM((2, mesh_rows // 2, chans // 2), bf16),
+            pltpu.VMEM((peers, mesh_rows, chans // 2), bf16),
+            pltpu.VMEM((grid_rows, chans // 2), f32),
+            dma((8,)), dma((5,)), dma((5,)), dma((2, peers)), dma((2, peers)),
+            dma((lines,)), dma((lines,)), dma((peers,)), dma((peers,)), dma((peers,)),
+            dma((lines, 2)), dma((lines, 2)), dma((2,)), dma((2,)), dma((1,)), dma((1,)),
+            dma((lines,)), dma((lines,)),
+        ],
+        compiler_params=pltpu.CompilerParams(collective_id=0, has_side_effects=True),
+    )(grid_state, w_src, bias_src[None, :], mesh_embed, w_node, w_dec, src, dst)
+
+
+def held_bytes(peers, grid_state, mesh_embed, *rest):
+    grid_rows, chans = grid_state.shape
+    mesh_rows = mesh_embed.shape[0]
+    return 2 * peers * grid_rows * (chans + 2 * mesh_rows)
+
+
+def per_device(grid_state, w_src, bias_src, mesh_embed, *rest):
+    peers = lax.axis_size("graph")
+    fits = (
+        peers % 2 == 0
+        and peers >= 4
+        and lax.axis_size("chan") == 2
+        and held_bytes(peers, grid_state, mesh_embed) <= VMEM_BUDGET
+    )
+    body = fused if fits else on_device
+    return body(grid_state, w_src, bias_src, mesh_embed, *rest)
+
+
 def solution(mesh):
     placed = (
         P(("member", "graph"), None),
@@ -88,7 +426,7 @@
         P(),
     )
     return jax.shard_map(
-        on_device,
+        per_device,
         mesh=mesh,
         in_specs=placed,
         out_specs=P(("member", "graph"), "chan"),

time: 228 us -> 75.1 us (0.33)
  waiting for transfers between devices: 79.5 us -> 0 us
  Pallas kernels: 0 us -> 70.8 us
  blocking collectives: 55.4 us -> 0 us
  local copies, waits for them, and re-layouts: 40.2 us -> 2.55 us
  matrix products: 25.6 us -> 0 us
  between operations: 13.3 us -> 0.02 us
  other arithmetic: 7.66 us -> 1.52 us
  starting transfers between devices: 5.81 us -> 0 us
    pallas_call x0 -> x1, Pallas kernels: none -> 70.8 us  [fused(): pl.pallas_call(functools.partial(graph_kernel, peers), out_shape=jax.Shap...]
    all_to_all x1 -> x0, blocking collectives: 55.4 us -> none  [on_device(): lax.all_to_all(picked, 'graph', split_axis=0, concat_axis=0, tiled=True)]
    all_to_all x1 -> x0, waiting for transfers between devices: 48.7 us -> none  [on_device(): lax.all_to_all(returned, 'graph', split_axis=0, concat_axis=0, tiled=True)]
    gather x2 -> x0, local copies, waits for them, and re-layouts: 38.1 us -> none  [the longest x1 24 us: on_device(): jnp.take(projected, dst_rows, axis=0)]
    dot_general x11 -> x0, matrix products: 25.6 us -> none  [the longest x8 15.9 us: add_block(): jnp.dot(one_hot, piece_vals, preferred_element_type=jnp.float32)]
    reduce_scatter x2 -> x0, waiting for transfers between devices: 19.3 us -> none  [the longest x1 9.86 us: on_device(): lax.psum_scatter(partial_hidden, 'chan', scatter_dimension=1, tiled=True)]
    all_gather x1 -> x0, waiting for transfers between devices: 11.4 us -> none  [on_device(): joined = lax.all_gather(arrived, 'chan', axis=1, tiled=True)]
    all_to_all x1 -> x0, starting transfers between devices: 5.72 us -> none  [on_device(): lax.all_to_all(returned, 'graph', split_axis=0, concat_axis=0, tiled=True)]
  transfers between devices with their start and end apart: 4 -> 0, of which waited for: 4 -> 0; matrix products, arithmetic and copies ran while one was open for 0% -> 0% of each run, Pallas kernels for 0% -> 0%
where the time goes in v1:
time: 75.1 us; the launch traced here: 74.9 us
  Pallas kernels  70.8 us (94%)
  local copies, waits for them, and re-layouts  2.55 us (3%)
  other arithmetic  1.52 us (2%)
    pallas_call x1, Pallas kernels, fused(): pl.pallas_call(functools.partial(graph_kernel, peers), out_shape=jax.Shap...  70.8 us
    unnamed x3, local copies, waits for them, and re-layouts  2.36 us
    select_n x1, other arithmetic, fused(): jnp.where(positions < received[:, None], slot_dst[:, 0, :], -1)[:, None, :]  1.52 us

profile of v1, /device:TPU:0, one launch (start us, length us, event | category | flops | bytes accessed | tf_op | source)
XLA Modules:
  0.0 74.9 jit_solution(14270500528679968441)
XLA Ops:
  0.0 0.0 copy-start
  0.0 0.7 copy-done
  0.7 0.2 dynamic-slice_reduce_fusion
  0.9 1.5 %compare_select_fusion = (s32[8,1,1024]{2,1,0:T(1,128)}, s32[8,1,1024]{2,1,0:T(1,128)}) fusion(s32[8,1,1024]{2,1,0:T(1,128)} %param.16, s32[8]{0:T(128)S(1)} %dynamic-slice_reduce_fusion, s32[1,8,1024]{2,1,0:T(8,128)} %param.15, s32[8]{0:T(128)S(1)} %dynamic-slice_bitcast_fusion), kind=kLoop, calls=%fused_computation | loop fusion | flops 32768 | bytes 131136 | tf_op jit(solution)/shard_map/jit(_where)/select_n | solution.py:359
  2.4 70.8 %shard_map.91 = bf16[1024,128]{1,0:T(8,128)(2,1)} custom-call(bf16[1024,256]{1,0:T(8,128)(2,1)} %x_ref.1, bf16[256,256]{1,0:T(8,128)(2,1)} %w_src_ref.1, f32[1,256]{1,0:T(1,128)} %bitcast.3, bf16[640,256]{1,0:T(8,128)(2,1)} %embed_ref.1, bf16[256,512]{1,0:T(8,128)(2,1)} %w_node_ref.1, bf16[256,256]{1,0:T(8,128)(2,1)} %w_dec_ref.1, ...), custom_call_target="tpu_custom_call" | custom-call | tf_op jit(solution)/shard_map/pallas_call | solution.py:368
  73.2 1.7 %copy.11 = bf16[1024,128]{1,0:T(8,128)(2,1)} copy(bf16[1024,128]{1,0:T(8,128)(2,1)} %shard_map.91) | data formatting | bytes 524288
  (1 shorter events, 0.0 us)
Async XLA Ops:
  0.0 0.7 copy-start

commit v2 on v1

v2 whole, which is shorter than its diff:
```python
import functools
import math

import jax
import jax.numpy as jnp
from jax import lax
from jax.experimental import pallas as pl
from jax.experimental.pallas import tpu as pltpu
from jax.sharding import PartitionSpec as P

CHUNKS = 2
VMEM_BUDGET = 48 * 2**20
MESH = pl.DeviceIdType.MESH
NT = (((1,), (1,)), ((), ()))


def edge_network(source_rows, w_src, bias_src):
    return jax.nn.silu(
        jnp.dot(source_rows, w_src, preferred_element_type=jnp.float32) + bias_src
    ).astype(jnp.bfloat16)


def segment_rows(values, indices, usable, row_count):
    slot_total = values.shape[0]
    width = values.shape[1]
    block_len = math.gcd(slot_total, 2048)
    block_count = slot_total // block_len
    targets = jnp.where(usable, indices, -1).reshape(block_count, block_len)
    pieces = values.reshape(block_count, block_len, width)
    row_ids = jnp.arange(row_count, dtype=jnp.int32)

    def add_block(summed, scan_item):
        row_target, piece_vals = scan_item
        one_hot = (row_ids[:, None] == row_target[None, :]).astype(jnp.bfloat16)
        return (summed + jnp.dot(one_hot, piece_vals, preferred_element_type=jnp.float32), None)

    result, unused = lax.scan(
        add_block, jnp.zeros((row_count, width), jnp.float32), (targets, pieces)
    )
    return result


def on_device(
    grid_state, w_src, bias_src, mesh_embed, w_node, w_dec, slot_src, slot_dst, slot_count
):
    peers = lax.axis_size("graph")
    own_index = lax.axis_index("graph")
    core_index = lax.axis_index("chan")
    capacity = slot_src.shape[2]
    positions = jnp.arange(capacity, dtype=jnp.int32)
    grid_rows = grid_state.shape[0]
    mesh_rows = mesh_embed.shape[0]
    sent_counts = lax.dynamic_slice_in_dim(slot_count, own_index, 1, 0)[0]
    recv_counts = lax.dynamic_slice_in_dim(slot_count, own_index, 1, 1)[:, 0]
    half_slots = capacity // 2
    chosen = lax.dynamic_slice_in_dim(slot_src[0], core_index * half_slots, half_slots, 1)
    picked = jnp.take(grid_state, chosen.reshape(-1), axis=0).reshape(
        peers, half_slots, grid_state.shape[1]
    )
    arrived = lax.all_to_all(picked, "graph", split_axis=0, concat_axis=0, tiled=True)
    joined = lax.all_gather(arrived, "chan", axis=1, tiled=True)
    messages = edge_network(joined.reshape(peers * capacity, grid_state.shape[1]), w_src, bias_src)
    arrive_ok = (positions[None, :] < recv_counts[:, None]).reshape(-1)
    dst_rows = slot_dst[:, 0, :].reshape(-1)
    aggregate = segment_rows(messages, dst_rows, arrive_ok, mesh_rows)
    partial_hidden = jnp.dot(
        aggregate.astype(jnp.bfloat16), w_node, preferred_element_type=jnp.float32
    )
    hidden_pre = lax.psum_scatter(partial_hidden, "chan", scatter_dimension=1, tiled=True)
    latent = (mesh_embed.astype(jnp.float32) + jax.nn.silu(hidden_pre)).astype(jnp.bfloat16)
    partial_proj = jnp.dot(latent, w_dec, preferred_element_type=jnp.float32)
    projected = lax.psum_scatter(partial_proj, "chan", scatter_dimension=1, tiled=True).astype(
        jnp.bfloat16
    )
    returned = jnp.take(projected, dst_rows, axis=0).reshape(peers, capacity, projected.shape[1])
    came_back = lax.all_to_all(returned, "graph", split_axis=0, concat_axis=0, tiled=True).reshape(
        peers * capacity, projected.shape[1]
    )
    send_ok = (positions[None, :] < sent_counts[:, None]).reshape(-1)
    decoded = segment_rows(came_back, slot_src[0].reshape(-1), send_ok, grid_rows)
    width_half = decoded.shape[1]
    own_cols = lax.dynamic_slice_in_dim(grid_state, core_index * width_half, width_half, 1)
    return (own_cols.astype(jnp.float32) + decoded).astype(jnp.bfloat16)


def silu(v):
    half = 0.5 * v
    return half + half * jnp.tanh(half)


def one_hot(first, rows, indices):
    row_ids = lax.broadcasted_iota(jnp.int32, (rows, indices.shape[1]), 0) + first
    return jnp.where(row_ids == indices, 1.0, 0.0).astype(jnp.bfloat16)


def graph_kernel(
    peers,
    x_ref, w_src_ref, bias_ref, embed_ref, w_node_ref, w_dec_ref, src_ref, dst_ref, count_ref,
    out_ref,
    x_all, src_own, src_in, dst_in, w_src_all, bias_all, embed_all, w_node_all, w_dec_all,
    enc, dec, hot, agg, proj, proj_all, total,
    local_sem, par_send, par_recv, idx_send, idx_recv,
    xo_send, xz_send, xy_send, x_recv, xm_send, xm_recv,
    po_send, pz_send, py_send, p_recv, pm_send, pm_recv,
):
    lines = peers // 2
    me = lax.axis_index("graph")
    core = lax.axis_index("chan")
    mate = 1 - core
    line, side = me // 2, me % 2
    other = line * 2 + (1 - side)
    grid_rows, chans = x_ref.shape
    half_grid = grid_rows // 2
    piece = half_grid // CHUNKS
    mesh_rows = embed_ref.shape[0]
    half_mesh = mesh_rows // 2
    cols = chans // 2
    tile = enc.shape[3]
    tiles = grid_rows // tile
    capacity = src_ref.shape[2]

    def remote(src, dst, send, recv, graph, chan):
        return pltpu.make_async_remote_copy(
            src_ref=src, dst_ref=dst, send_sem=send, recv_sem=recv,
            device_id={"graph": graph, "chan": chan}, device_id_type=MESH,
        )

    barrier = pltpu.get_barrier_semaphore()
    for step in range(peers):
        for chan in range(2):
            if step == 0 and chan == 0:
                continue
            pl.semaphore_signal(
                barrier, inc=1,
                device_id={"graph": (me + step) % peers, "chan": (core + chan) % 2},
                device_id_type=MESH,
            )
    slots = lax.broadcasted_iota(jnp.int32, (1, capacity), 1)
    for to in range(peers):
        src_own[to] = jnp.where(slots < count_ref[me, to], src_ref[0, to : to + 1, :], -1)
    my_rows = pl.ds(pl.multiple_of(core * half_mesh, half_mesh), half_mesh)
    mate_rows = pl.ds(pl.multiple_of(mate * half_mesh, half_mesh), half_mesh)
    locals_ = [
        pltpu.make_async_copy(x_ref, x_all.at[me], local_sem.at[0]),
        pltpu.make_async_copy(w_src_ref, w_src_all.at[core], local_sem.at[1]),
        pltpu.make_async_copy(bias_ref, bias_all.at[core], local_sem.at[2]),
        pltpu.make_async_copy(embed_ref.at[my_rows], embed_all.at[core], local_sem.at[3]),
        pltpu.make_async_copy(w_node_ref, w_node_all.at[core], local_sem.at[4]),
        pltpu.make_async_copy(w_dec_ref, w_dec_all.at[core], local_sem.at[5]),
        pltpu.make_async_copy(src_own.at[me], src_in.at[me], local_sem.at[6]),
        pltpu.make_async_copy(dst_ref.at[me], dst_in.at[me], local_sem.at[7]),
    ]
    for copy in locals_:
        copy.start()
    pl.semaphore_wait(barrier, 2 * peers - 1)

    sends = []
    idx_copies = []
    for step in range(1, peers):
        to = (me + step) % peers
        for at, (ref, into) in enumerate(((src_own, src_in), (dst_ref, dst_in))):
            copy = remote(
                ref.at[to], into.at[me], idx_send.at[at, step], idx_recv.at[at, step], to, core
            )
            copy.start()
            idx_copies.append(copy)

    def nearest(at):
        return sorted((p for p in range(lines) if p != at), key=lambda p: (abs(p - at), p))

    from_line = [
        sum(jnp.where(line == at, nearest(at)[i], 0) for at in range(lines))
        for i in range(lines - 1)
    ]
    up, down = (line + 1) * 2 + side, (line - 1) * 2 + side

    def along(source, make):
        for going, target in (
            ((source <= line) & (line < lines - 1), up),
            ((source >= line) & (line > 0), down),
        ):
            @pl.when(going)
            def _(target=target):
                make(target).start()
            sends.append((going, functools.partial(make, target)))

    def begin(copy):
        copy.start()
        sends.append((None, lambda: copy))

    def x_part(shard, half, c):
        first = pl.multiple_of(half * half_grid, half_grid) + c * piece
        return x_all.at[shard, pl.ds(pl.multiple_of(first, piece), piece)]

    def x_own(c):
        first = pl.multiple_of(core * half_grid, half_grid) + c * piece
        return x_ref.at[pl.ds(pl.multiple_of(first, piece), piece)]

    for c in range(CHUNKS):
        begin(remote(x_own(c), x_part(me, core, c), xy_send.at[line, c], x_recv.at[1, line, c], other, core))
        for at, (going, target) in enumerate(((line < lines - 1, up), (line > 0, down))):
            def make(c=c, at=at, target=target):
                return remote(
                    x_own(c), x_part(me, core, c), xo_send.at[at, c], x_recv.at[0, line, c],
                    target, core,
                )
            @pl.when(going)
            def _(make=make):
                make().start()
            sends.append((going, make))

    par_copies = [
        remote(w_src_ref, w_src_all.at[core], par_send.at[0], par_recv.at[0], me, mate),
        remote(bias_ref, bias_all.at[core], par_send.at[1], par_recv.at[1], me, mate),
        remote(embed_ref.at[mate_rows], embed_all.at[core], par_send.at[2], par_recv.at[2], me, mate),
        remote(w_node_ref, w_node_all.at[core], par_send.at[3], par_recv.at[3], me, mate),
        remote(w_dec_ref, w_dec_all.at[core], par_send.at[4], par_recv.at[4], me, mate),
    ]
    for copy in par_copies:
        copy.start()

    def to_mate(flip, source, c, shard):
        ref = x_part(shard, core, c)
        begin(remote(ref, ref, xm_send.at[flip, source, c], xm_recv.at[flip, source, c], me, mate))

    def relay(i, c):
        source = from_line[i]
        shard = source * 2 + side
        ref = x_part(shard, core, c)
        remote(ref, ref, xz_send.at[source, c], x_recv.at[0, source, c], me, mate).wait_recv()
        along(source, lambda target: remote(
            ref, ref, xz_send.at[source, c], x_recv.at[0, source, c], target, core))
        begin(remote(ref, ref, xy_send.at[source, c], x_recv.at[1, source, c], other, core))
        to_mate(0, source, c, shard)

    def take(source, c):
        shard = source * 2 + (1 - side)
        ref = x_part(shard, core, c)
        remote(ref, ref, xz_send.at[source, c], x_recv.at[1, source, c], me, mate).wait_recv()
        to_mate(1, source, c, shard)

    def build_enc(shard, carry):
        hot[: half_mesh, :] = one_hot(core * half_mesh, half_mesh, dst_ref[shard])
        for t in range(tiles):
            picks = one_hot(t * tile, tile, src_in[shard])
            enc[shard, t] = lax.dot_general(
                hot[: half_mesh, :], picks, NT, preferred_element_type=jnp.float32
            ).astype(jnp.bfloat16)
        return carry

    def build_dec(shard, carry):
        hot[...] = one_hot(0, mesh_rows, dst_in[shard])
        for t in range(grid_rows // 256):
            picks = one_hot(t * 256, 256, src_own[shard])
            dec[shard, t * 256 : (t + 1) * 256, :] = lax.dot_general(
                picks, hot[...], NT, preferred_element_type=jnp.float32
            ).astype(jnp.bfloat16)
        return carry

    done = {build_enc: 0, build_dec: 0}

    def build(which, count):
        first = done[which]
        last = min(first + count, peers)
        if last > first:
            lax.fori_loop(first, last, which, 0)
        done[which] = last

    def encode(shard):
        def step(t, carry):
            rows = pl.ds(pl.multiple_of(t * tile, tile), tile)
            for h in range(2):
                pre = jnp.dot(
                    x_all[shard, rows, :], w_src_all[h], preferred_element_type=jnp.float32
                ) + bias_all[h]
                agg[h] += jnp.dot(
                    enc[shard, t], silu(pre).astype(jnp.bfloat16),
                    preferred_element_type=jnp.float32,
                )
            return carry
        lax.fori_loop(0, tiles, step, 0)

    def encode_from(flip, source):
        shard = source * 2 + (side if flip == 0 else 1 - side)
        for c in range(CHUNKS):
            ref = x_part(shard, mate, c)
            remote(ref, ref, xm_send.at[flip, source, c], xm_recv.at[flip, source, c], me, mate).wait_recv()
        encode(shard)

    for copy in locals_:
        copy.wait()
    for copy in idx_copies:
        copy.wait()
    agg[...] = jnp.zeros_like(agg)
    total[...] = x_ref[:, pl.ds(pl.multiple_of(core * cols, cols), cols)].astype(jnp.float32)
    build(build_enc, peers * 3 // 8)
    last = lines - 2
    for i in range(lines - 1):
        for c in range(CHUNKS):
            relay(i, c)
            if i == 0:
                build(build_enc, peers // CHUNKS // 4)
            else:
                take(from_line[i - 1], c)
                if c < CHUNKS - 1:
                    build(build_dec, 1)
        if i == 0:
            for c in range(CHUNKS):
                take(line, c)
            for copy in par_copies:
                copy.wait()
            build(build_enc, peers)
            encode(me)
        elif i == 1:
            encode_from(0, from_line[0])
            encode_from(1, line)
            build(build_dec, 1)
        else:
            encode_from(0, from_line[i - 1])
            encode_from(1, from_line[i - 2])
            build(build_dec, 1)
    encode_from(0, from_line[last])
    encode_from(1, from_line[last - 1])
    for c in range(CHUNKS):
        take(from_line[last], c)
    encode_from(1, from_line[last])

    hidden = sum(
        jnp.dot(agg[h].astype(jnp.bfloat16), w_node_all[h], preferred_element_type=jnp.float32)
        for h in range(2)
    )
    width = hidden.shape[1] // 2
    projected = sum(
        jnp.dot(
            (
                embed_all[h].astype(jnp.float32) + silu(hidden[:, h * width : (h + 1) * width])
            ).astype(jnp.bfloat16),
            w_dec_all[h], preferred_element_type=jnp.float32,
        )
        for h in range(2)
    ).astype(jnp.bfloat16)
    for h in range(2):
        proj[h] = projected[:, h * cols : (h + 1) * cols]

    own_copy = pltpu.make_async_copy(proj.at[core], proj_all.at[me, my_rows], local_sem.at[0])
    own_copy.start()
    into = proj_all.at[me, my_rows]
    for flip in range(2):
        chan = (core + flip) % 2
        begin(remote(proj.at[chan], into, py_send.at[line, flip], p_recv.at[1, line, core], other, chan))
        for at, (going, target) in enumerate(((line < lines - 1, up), (line > 0, down))):
            def make(flip=flip, chan=chan, at=at, target=target):
                return remote(
                    proj.at[chan], into, po_send.at[at, flip], p_recv.at[0, line, core],
                    target, chan,
                )
            @pl.when(going)
            def _(make=make):
                make().start()
            sends.append((going, make))
    begin(remote(proj.at[mate], into, pm_send.at[0], pm_recv.at[0], me, mate))

    def p_part(shard, half):
        return proj_all.at[shard, half * half_mesh : (half + 1) * half_mesh]

    def p_wait(flip, source, half):
        ref = p_part(source * 2 + (side if flip == 0 else 1 - side), half)
        remote(ref, ref, pz_send.at[source, half], p_recv.at[flip, source, half], me, mate).wait_recv()

    def p_relay(i):
        source = from_line[i]
        for half in range(2):
            p_wait(0, source, half)
            ref = p_part(source * 2 + side, half)
            along(source, lambda target, half=half, ref=ref: remote(
                ref, ref, pz_send.at[source, half], p_recv.at[0, source, half], target, core))
            begin(remote(ref, ref, py_send.at[source, half], p_recv.at[1, source, half], other, core))

    def decode(shard):
        def step(t, carry):
            rows = pl.ds(pl.multiple_of(t * half_grid, half_grid), half_grid)
            total[rows, :] += jnp.dot(
                dec[shard, rows, :], proj_all[shard], preferred_element_type=jnp.float32
            )
            return carry
        lax.fori_loop(0, 2, step, 0)

    left = peers - done[build_dec]
    for i in range(lines - 1):
        build(build_dec, -(-left // (lines - 1)))
        p_relay(i)
    own_copy.wait()
    remote(proj.at[mate], into, pm_send.at[0], pm_recv.at[0], me, mate).wait_recv()
    decode(me)
    for i in range(lines - 1):
        decode(from_line[i] * 2 + side)
    for source in [line] + from_line:
        for half in range(2):
            p_wait(1, source, half)
        decode(source * 2 + 1 - side)
    out_ref[...] = total[...].astype(jnp.bfloat16)

    for going, make in sends:
        if going is None:
            make().wait_send()
        else:
            @pl.when(going)
            def _(make=make):
                make().wait_send()


def fused(grid_state, w_src, bias_src, mesh_embed, w_node, w_dec, slot_src, slot_dst, slot_count):
    peers = lax.axis_size("graph")
    capacity = slot_src.shape[2]
    grid_rows, chans = grid_state.shape
    mesh_rows = mesh_embed.shape[0]
    hidden = w_src.shape[1]
    lines = peers // 2
    bf16, f32 = jnp.bfloat16, jnp.float32
    dma = pltpu.SemaphoreType.DMA
    vmem = pl.BlockSpec(memory_space=pltpu.VMEM)
    tile = grid_rows // 2
    return pl.pallas_call(
        functools.partial(graph_kernel, peers),
        out_shape=jax.ShapeDtypeStruct((grid_rows, chans // 2), bf16),
        in_specs=[vmem] * 8 + [pl.BlockSpec(memory_space=pltpu.SMEM)],
        out_specs=vmem,
        scratch_shapes=[
            pltpu.VMEM((peers, grid_rows, chans), bf16),
            pltpu.VMEM((peers, 1, capacity), jnp.int32),
            pltpu.VMEM((peers, 1, capacity), jnp.int32),
            pltpu.VMEM((peers, 1, capacity), jnp.int32),
            pltpu.VMEM((2,) + w_src.shape, bf16),
            pltpu.VMEM((2, 1, hidden), f32),
            pltpu.VMEM((2, mesh_rows // 2, hidden), bf16),
            pltpu.VMEM((2,) + w_node.shape, bf16),
            pltpu.VMEM((2,) + w_dec.shape, bf16),
            pltpu.VMEM((peers, grid_rows // tile, mesh_rows // 2, tile), bf16),
            pltpu.VMEM((peers, grid_rows, mesh_rows), bf16),
            pltpu.VMEM((mesh_rows, capacity), bf16),
            pltpu.VMEM((2, mesh_rows // 2, hidden), f32),
            pltpu.VMEM((2, mesh_rows // 2, chans // 2), bf16),
            pltpu.VMEM((peers, mesh_rows, chans // 2), bf16),
            pltpu.VMEM((grid_rows, chans // 2), f32),
            dma((8,)), dma((5,)), dma((5,)), dma((2, peers)), dma((2, peers)),
            dma((2, CHUNKS)), dma((lines, CHUNKS)), dma((lines, CHUNKS)), dma((2, lines, CHUNKS)),
            dma((2, lines, CHUNKS)), dma((2, lines, CHUNKS)),
            dma((2, 2)), dma((lines, 2)), dma((lines, 2)), dma((2, lines, 2)), dma((1,)), dma((1,)),
        ],
        compiler_params=pltpu.CompilerParams(collective_id=0, has_side_effects=True),
    )(grid_state, w_src, bias_src[None, :], mesh_embed, w_node, w_dec, slot_src, slot_dst, slot_count)


def held_bytes(peers, grid_state, mesh_embed, *rest):
    grid_rows, chans = grid_state.shape
    mesh_rows = mesh_embed.shape[0]
    return 2 * peers * grid_rows * (chans + 2 * mesh_rows)


def per_device(grid_state, w_src, bias_src, mesh_embed, *rest):
    peers = lax.axis_size("graph")
    fits = (
        peers % 2 == 0
        and peers >= 4
        and lax.axis_size("chan") == 2
        and held_bytes(peers, grid_state, mesh_embed) <= VMEM_BUDGET
    )
    body = fused if fits else on_device
    return body(grid_state, w_src, bias_src, mesh_embed, *rest)


def solution(mesh):
    placed = (
        P(("member", "graph"), None),
        P(None, "chan"),
        P("chan"),
        P("graph", "chan"),
        P("chan", None),
        P("chan", None),
        P("graph", None, None),
        P(None, "graph", None),
        P(),
    )
    return jax.shard_map(
        per_device,
        mesh=mesh,
        in_specs=placed,
        out_specs=P(("member", "graph"), "chan"),
        check_vma=False,
    )
```

time: 75.1 us -> 75.1 us (level)
  Pallas kernels: 70.8 us -> 73.3 us
  other arithmetic: 1.52 us -> 0 us
  local copies, waits for them, and re-layouts: 2.55 us -> 1.67 us
    pallas_call x1, Pallas kernels: 70.8 us -> 73.3 us  [fused(): pl.pallas_call(functools.partial(graph_kernel, peers), out_shape=jax.Shap...]
    select_n x1 -> x0, other arithmetic: 1.52 us -> none  [fused(): jnp.where(positions < received[:, None], slot_dst[:, 0, :], -1)[:, None, :]]
    unnamed x3 -> x1, local copies, waits for them, and re-layouts: 2.36 us -> 1.67 us
where the time goes in v2:
time: 75.1 us; the launch traced here: 75 us
  Pallas kernels  73.3 us (98%)
  local copies, waits for them, and re-layouts  1.67 us (2%)
    pallas_call x1, Pallas kernels, fused(): pl.pallas_call(functools.partial(graph_kernel, peers), out_shape=jax.Shap...  73.3 us
    unnamed x1, local copies, waits for them, and re-layouts  1.67 us

profile of v2, /device:TPU:0, one launch (start us, length us, event | category | flops | bytes accessed | tf_op | source)
XLA Modules:
  0.0 75.0 jit_solution(269458840086660627)
XLA Ops:
  0.0 73.3 %shard_map.91 = bf16[1024,128]{1,0:T(8,128)(2,1)} custom-call(bf16[1024,256]{1,0:T(8,128)(2,1)} %x_ref.1, bf16[256,256]{1,0:T(8,128)(2,1)} %w_src_ref.1, f32[1,256]{1,0:T(1,128)} %bitcast.1, bf16[640,256]{1,0:T(8,128)(2,1)} %embed_ref.1, bf16[256,512]{1,0:T(8,128)(2,1)} %w_node_ref.1, bf16[256,256]{1,0:T(8,128)(2,1)} %w_dec_ref.1, s32[1,8,1024]{2,1,0:T(8,128)} %src_ref.1, ...), custom_call_target="tpu_custom_call" | custom-call | tf_op jit(solution)/shard_map/pallas_call | solution.py:423
  73.3 1.7 %copy.11 = bf16[1024,128]{1,0:T(8,128)(2,1)} copy(bf16[1024,128]{1,0:T(8,128)(2,1)} %shard_map.91) | data formatting | bytes 524288

commit v3 on v2

--- a/solution.py
+++ b/solution.py
@@ -9,6 +9,7 @@
 from jax.sharding import PartitionSpec as P
 
 CHUNKS = 2
+HOT = jnp.float8_e4m3fn
 VMEM_BUDGET = 48 * 2**20
 MESH = pl.DeviceIdType.MESH
 NT = (((1,), (1,)), ((), ()))
@@ -90,7 +91,7 @@
 
 def one_hot(first, rows, indices):
     row_ids = lax.broadcasted_iota(jnp.int32, (rows, indices.shape[1]), 0) + first
-    return jnp.where(row_ids == indices, 1.0, 0.0).astype(jnp.bfloat16)
+    return jnp.where(row_ids == indices, 1.0, 0.0).astype(HOT)
 
 
 def graph_kernel(
@@ -101,7 +102,7 @@
     enc, dec, hot, agg, proj, proj_all, total,
     local_sem, par_send, par_recv, idx_send, idx_recv,
     xo_send, xz_send, xy_send, x_recv, xm_send, xm_recv,
-    po_send, pz_send, py_send, p_recv, pm_send, pm_recv,
+    po_send, pz_send, py_send, p_recv, pm_send, pm_recv, dec_send, dec_recv,
 ):
     lines = peers // 2
     me = lax.axis_index("graph")
@@ -239,7 +240,8 @@
         remote(ref, ref, xz_send.at[source, c], x_recv.at[1, source, c], me, mate).wait_recv()
         to_mate(1, source, c, shard)
 
-    def build_enc(shard, carry):
+    def build_enc(i, carry):
+        shard = (me + i) % peers
         hot[: half_mesh, :] = one_hot(core * half_mesh, half_mesh, dst_ref[shard])
         for t in range(tiles):
             picks = one_hot(t * tile, tile, src_in[shard])
@@ -248,22 +250,37 @@
             ).astype(jnp.bfloat16)
         return carry
 
-    def build_dec(shard, carry):
+    def build_dec(i, carry):
+        shard = (me + i) % peers
         hot[...] = one_hot(0, mesh_rows, dst_in[shard])
-        for t in range(grid_rows // 256):
-            picks = one_hot(t * 256, 256, src_own[shard])
-            dec[shard, t * 256 : (t + 1) * 256, :] = lax.dot_general(
+        for t in range(half_grid // 256):
+            first = pl.multiple_of(core * half_grid, half_grid) + t * 256
+            picks = one_hot(first, 256, src_own[shard])
+            dec[shard, pl.ds(pl.multiple_of(first, 256), 256), :] = lax.dot_general(
                 picks, hot[...], NT, preferred_element_type=jnp.float32
             ).astype(jnp.bfloat16)
         return carry
 
     done = {build_enc: 0, build_dec: 0}
+    pending = []
+
+    def dec_copy(i, half):
+        shard = (me + i) % peers
+        ref = dec.at[shard, pl.ds(pl.multiple_of(half * half_grid, half_grid), half_grid)]
+        return remote(ref, ref, dec_send.at[shard], dec_recv.at[shard], me, mate)
+
+    def flush():
+        while pending:
+            begin(dec_copy(pending.pop(0), core))
 
     def build(which, count):
         first = done[which]
         last = min(first + count, peers)
         if last > first:
+            flush()
             lax.fori_loop(first, last, which, 0)
+            if which is build_dec:
+                pending.extend(range(first, last))
         done[which] = last
 
     def encode(shard):
@@ -289,11 +306,17 @@
 
     for copy in locals_:
         copy.wait()
+    agg[...] = jnp.zeros_like(agg)
+    total[...] = x_ref[:, pl.ds(pl.multiple_of(core * cols, cols), cols)].astype(jnp.float32)
+    build(build_enc, 1)
+    build(build_dec, 1)
+    for copy in par_copies:
+        copy.wait()
+    encode(me)
     for copy in idx_copies:
         copy.wait()
-    agg[...] = jnp.zeros_like(agg)
-    total[...] = x_ref[:, pl.ds(pl.multiple_of(core * cols, cols), cols)].astype(jnp.float32)
-    build(build_enc, peers * 3 // 8)
+    flush()
+    build(build_enc, peers // 4)
     last = lines - 2
     for i in range(lines - 1):
         for c in range(CHUNKS):
@@ -307,10 +330,7 @@
         if i == 0:
             for c in range(CHUNKS):
                 take(line, c)
-            for copy in par_copies:
-                copy.wait()
             build(build_enc, peers)
-            encode(me)
         elif i == 1:
             encode_from(0, from_line[0])
             encode_from(1, line)
@@ -385,10 +405,14 @@
             return carry
         lax.fori_loop(0, 2, step, 0)
 
+    flush()
     left = peers - done[build_dec]
     for i in range(lines - 1):
         build(build_dec, -(-left // (lines - 1)))
         p_relay(i)
+    flush()
+    for i in range(peers):
+        dec_copy(i, mate).wait_recv()
     own_copy.wait()
     remote(proj.at[mate], into, pm_send.at[0], pm_recv.at[0], me, mate).wait_recv()
     decode(me)
@@ -437,7 +461,7 @@
             pltpu.VMEM((2,) + w_dec.shape, bf16),
             pltpu.VMEM((peers, grid_rows // tile, mesh_rows // 2, tile), bf16),
             pltpu.VMEM((peers, grid_rows, mesh_rows), bf16),
-            pltpu.VMEM((mesh_rows, capacity), bf16),
+            pltpu.VMEM((mesh_rows, capacity), HOT),
             pltpu.VMEM((2, mesh_rows // 2, hidden), f32),
             pltpu.VMEM((2, mesh_rows // 2, chans // 2), bf16),
             pltpu.VMEM((peers, mesh_rows, chans // 2), bf16),
@@ -445,7 +469,7 @@
             dma((8,)), dma((5,)), dma((5,)), dma((2, peers)), dma((2, peers)),
             dma((2, CHUNKS)), dma((lines, CHUNKS)), dma((lines, CHUNKS)), dma((2, lines, CHUNKS)),
             dma((2, lines, CHUNKS)), dma((2, lines, CHUNKS)),
-            dma((2, 2)), dma((lines, 2)), dma((lines, 2)), dma((2, lines, 2)), dma((1,)), dma((1,)),
+            dma((2, 2)), dma((lines, 2)), dma((lines, 2)), dma((2, lines, 2)), dma((1,)), dma((1,)), dma((peers,)), dma((peers,)),
         ],
         compiler_params=pltpu.CompilerParams(collective_id=0, has_side_effects=True),
     )(grid_state, w_src, bias_src[None, :], mesh_embed, w_node, w_dec, slot_src, slot_dst, slot_count)

time: 75.1 us -> 67.4 us (0.90)
  the two profiles are of different devices: /device:TPU:0 before, /device:TPU:1 now
where the time goes in v3:
time: 67.4 us; the launch traced here: 67.2 us
  Pallas kernels  65.5 us (97%)
  local copies, waits for them, and re-layouts  1.67 us (2%)
    pallas_call x1, Pallas kernels, fused(): pl.pallas_call(functools.partial(graph_kernel, peers), out_shape=jax.Shap...  65.5 us
    unnamed x1, local copies, waits for them, and re-layouts  1.67 us

profile of v3, /device:TPU:1, one launch (start us, length us, event | category | flops | bytes accessed | tf_op | source)
XLA Modules:
  0.0 67.2 jit_solution(4032048465917718953)
XLA Ops:
  0.0 65.5 %shard_map.91 = bf16[1024,128]{1,0:T(8,128)(2,1)} custom-call(bf16[1024,256]{1,0:T(8,128)(2,1)} %x_ref.1, bf16[256,256]{1,0:T(8,128)(2,1)} %w_src_ref.1, f32[1,256]{1,0:T(1,128)} %bitcast.1, bf16[640,256]{1,0:T(8,128)(2,1)} %embed_ref.1, bf16[256,512]{1,0:T(8,128)(2,1)} %w_node_ref.1, bf16[256,256]{1,0:T(8,128)(2,1)} %w_dec_ref.1, s32[1,8,1024]{2,1,0:T(8,128)} %src_ref.1, ...), custom_call_target="tpu_custom_call" | custom-call | tf_op jit(solution)/shard_map/pallas_call | solution.py:447
  65.6 1.7 %copy.11 = bf16[1024,128]{1,0:T(8,128)(2,1)} copy(bf16[1024,128]{1,0:T(8,128)(2,1)} %shard_map.91) | data formatting | bytes 524288

commit v4 on v3

--- a/solution.py
+++ b/solution.py
@@ -8,7 +8,7 @@
 from jax.experimental.pallas import tpu as pltpu
 from jax.sharding import PartitionSpec as P
 
-CHUNKS = 2
+CHUNKS = 4
 HOT = jnp.float8_e4m3fn
 VMEM_BUDGET = 48 * 2**20
 MESH = pl.DeviceIdType.MESH
@@ -99,7 +99,7 @@
     x_ref, w_src_ref, bias_ref, embed_ref, w_node_ref, w_dec_ref, src_ref, dst_ref, count_ref,
     out_ref,
     x_all, src_own, src_in, dst_in, w_src_all, bias_all, embed_all, w_node_all, w_dec_all,
-    enc, dec, hot, agg, proj, proj_all, total,
+    enc, dec, hot, agg, proj, proj_all,
     local_sem, par_send, par_recv, idx_send, idx_recv,
     xo_send, xz_send, xy_send, x_recv, xm_send, xm_recv,
     po_send, pz_send, py_send, p_recv, pm_send, pm_recv, dec_send, dec_recv,
@@ -153,6 +153,8 @@
     ]
     for copy in locals_:
         copy.start()
+    for copy in locals_:
+        copy.wait()
     pl.semaphore_wait(barrier, 2 * peers - 1)
 
     sends = []
@@ -195,7 +197,7 @@
 
     def x_own(c):
         first = pl.multiple_of(core * half_grid, half_grid) + c * piece
-        return x_ref.at[pl.ds(pl.multiple_of(first, piece), piece)]
+        return x_all.at[me, pl.ds(pl.multiple_of(first, piece), piece)]
 
     for c in range(CHUNKS):
         begin(remote(x_own(c), x_part(me, core, c), xy_send.at[line, c], x_recv.at[1, line, c], other, core))
@@ -211,11 +213,11 @@
             sends.append((going, make))
 
     par_copies = [
-        remote(w_src_ref, w_src_all.at[core], par_send.at[0], par_recv.at[0], me, mate),
-        remote(bias_ref, bias_all.at[core], par_send.at[1], par_recv.at[1], me, mate),
+        remote(w_src_all.at[core], w_src_all.at[core], par_send.at[0], par_recv.at[0], me, mate),
+        remote(bias_all.at[core], bias_all.at[core], par_send.at[1], par_recv.at[1], me, mate),
         remote(embed_ref.at[mate_rows], embed_all.at[core], par_send.at[2], par_recv.at[2], me, mate),
-        remote(w_node_ref, w_node_all.at[core], par_send.at[3], par_recv.at[3], me, mate),
-        remote(w_dec_ref, w_dec_all.at[core], par_send.at[4], par_recv.at[4], me, mate),
+        remote(w_node_all.at[core], w_node_all.at[core], par_send.at[3], par_recv.at[3], me, mate),
+        remote(w_dec_all.at[core], w_dec_all.at[core], par_send.at[4], par_recv.at[4], me, mate),
     ]
     for copy in par_copies:
         copy.start()
@@ -304,10 +306,8 @@
             remote(ref, ref, xm_send.at[flip, source, c], xm_recv.at[flip, source, c], me, mate).wait_recv()
         encode(shard)
 
-    for copy in locals_:
-        copy.wait()
     agg[...] = jnp.zeros_like(agg)
-    total[...] = x_ref[:, pl.ds(pl.multiple_of(core * cols, cols), cols)].astype(jnp.float32)
+    out_ref[...] = x_all[me, :, pl.ds(pl.multiple_of(core * cols, cols), cols)].astype(jnp.float32)
     build(build_enc, 1)
     build(build_dec, 1)
     for copy in par_copies:
@@ -340,8 +340,9 @@
             encode_from(1, from_line[i - 2])
             build(build_dec, 1)
     encode_from(0, from_line[last])
+    take(from_line[last], 0)
     encode_from(1, from_line[last - 1])
-    for c in range(CHUNKS):
+    for c in range(1, CHUNKS):
         take(from_line[last], c)
     encode_from(1, from_line[last])
 
@@ -381,7 +382,7 @@
     begin(remote(proj.at[mate], into, pm_send.at[0], pm_recv.at[0], me, mate))
 
     def p_part(shard, half):
-        return proj_all.at[shard, half * half_mesh : (half + 1) * half_mesh]
+        return proj_all.at[shard, pl.ds(pl.multiple_of(half * half_mesh, half_mesh), half_mesh)]
 
     def p_wait(flip, source, half):
         ref = p_part(source * 2 + (side if flip == 0 else 1 - side), half)
@@ -389,7 +390,7 @@
 
     def p_relay(i):
         source = from_line[i]
-        for half in range(2):
+        for half in (core, mate):
             p_wait(0, source, half)
             ref = p_part(source * 2 + side, half)
             along(source, lambda target, half=half, ref=ref: remote(
@@ -399,7 +400,7 @@
     def decode(shard):
         def step(t, carry):
             rows = pl.ds(pl.multiple_of(t * half_grid, half_grid), half_grid)
-            total[rows, :] += jnp.dot(
+            out_ref[rows, :] += jnp.dot(
                 dec[shard, rows, :], proj_all[shard], preferred_element_type=jnp.float32
             )
             return carry
@@ -419,10 +420,9 @@
     for i in range(lines - 1):
         decode(from_line[i] * 2 + side)
     for source in [line] + from_line:
-        for half in range(2):
+        for half in (core, mate):
             p_wait(1, source, half)
         decode(source * 2 + 1 - side)
-    out_ref[...] = total[...].astype(jnp.bfloat16)
 
     for going, make in sends:
         if going is None:
@@ -446,8 +446,8 @@
     tile = grid_rows // 2
     return pl.pallas_call(
         functools.partial(graph_kernel, peers),
-        out_shape=jax.ShapeDtypeStruct((grid_rows, chans // 2), bf16),
-        in_specs=[vmem] * 8 + [pl.BlockSpec(memory_space=pltpu.SMEM)],
+        out_shape=jax.ShapeDtypeStruct((grid_rows, chans // 2), f32),
+        in_specs=[pl.BlockSpec(memory_space=pl.ANY)] * 6 + [vmem] * 2 + [pl.BlockSpec(memory_space=pltpu.SMEM)],
         out_specs=vmem,
         scratch_shapes=[
             pltpu.VMEM((peers, grid_rows, chans), bf16),
@@ -465,14 +465,13 @@
             pltpu.VMEM((2, mesh_rows // 2, hidden), f32),
             pltpu.VMEM((2, mesh_rows // 2, chans // 2), bf16),
             pltpu.VMEM((peers, mesh_rows, chans // 2), bf16),
-            pltpu.VMEM((grid_rows, chans // 2), f32),
             dma((8,)), dma((5,)), dma((5,)), dma((2, peers)), dma((2, peers)),
             dma((2, CHUNKS)), dma((lines, CHUNKS)), dma((lines, CHUNKS)), dma((2, lines, CHUNKS)),
             dma((2, lines, CHUNKS)), dma((2, lines, CHUNKS)),
             dma((2, 2)), dma((lines, 2)), dma((lines, 2)), dma((2, lines, 2)), dma((1,)), dma((1,)), dma((peers,)), dma((peers,)),
         ],
         compiler_params=pltpu.CompilerParams(collective_id=0, has_side_effects=True),
-    )(grid_state, w_src, bias_src[None, :], mesh_embed, w_node, w_dec, slot_src, slot_dst, slot_count)
+    )(grid_state, w_src, bias_src[None, :], mesh_embed, w_node, w_dec, slot_src, slot_dst, slot_count).astype(bf16)
 
 
 def held_bytes(peers, grid_state, mesh_embed, *rest):

time: 67.4 us -> 66.7 us (0.990)
  the two profiles are of different devices: /device:TPU:1 before, /device:TPU:0 now
where the time goes in v4:
time: 66.7 us; the launch traced here: 66.4 us
  Pallas kernels  64.7 us (97%)
  other arithmetic  1.77 us (3%)
    pallas_call x1, Pallas kernels, fused(): pl.pallas_call(functools.partial(graph_kernel, peers), out_shape=jax.Shap...  64.7 us
    convert_element_type x1, other arithmetic, fused(): return pl.pallas_call(functools.partial(graph_kernel, peers), out_shape=j...  1.77 us

profile of v4, /device:TPU:0, one launch (start us, length us, event | category | flops | bytes accessed | tf_op | source)
XLA Modules:
  0.0 66.4 jit_solution(10397433791934457494)
XLA Ops:
  0.0 64.7 %shard_map.91 = f32[1024,128]{1,0:T(8,128)} custom-call(bf16[1024,256]{1,0:T(8,128)(2,1)} %x_ref.1, bf16[256,256]{1,0:T(8,128)(2,1)} %w_src_ref.1, f32[1,256]{1,0:T(1,128)} %bitcast.1, bf16[640,256]{1,0:T(8,128)(2,1)} %embed_ref.1, bf16[256,512]{1,0:T(8,128)(2,1)} %w_node_ref.1, bf16[256,256]{1,0:T(8,128)(2,1)} %w_dec_ref.1, s32[1,8,1024]{2,1,0:T(8,128)} %src_ref.1, ...), custom_call_target="tpu_custom_call" | custom-call | tf_op jit(solution)/shard_map/pallas_call | solution.py:447
  64.7 1.8 %convert_element_type.3 = bf16[1024,128]{1,0:T(8,128)(2,1)} convert(f32[1024,128]{1,0:T(8,128)} %shard_map.91) | non-fusion elementwise | flops 131072 | bytes 786432 | tf_op jit(solution)/shard_map/convert_element_type | solution.py:474
